TPU v7x, 32 devices: a whole 2x2x4 slice. The times are simulated.
32 devices in a mesh: data: 8 (over z, y), model: 4 (over x, core).
Axes of the slice: x: 2, y: 2, z: 4, core: 2. Of those that a mesh axis runs over, the one named last changes fastest.
Arguments:
- teacher_in: bfloat16 [32, 3072, 2048], P('data', 'model')
- student_in: bfloat16 [32, 3072, 512], P(('data', 'model'))
- teacher_gain: float32 [1, 2048], replicated
- teacher_up: bfloat16 [1, 2048, 8192], P(None, None, 'model')
- teacher_down: bfloat16 [1, 8192, 2048], P(None, 'model')
- student_gain: float32 [1, 512], replicated
- student_up: bfloat16 [1, 512, 2048], replicated
- student_down: bfloat16 [1, 2048, 512], replicated
- student_proj: bfloat16 [1, 2048, 512], replicated
Outputs:
- output 1: float32 [], replicated
- output 2: float32 [1, 512, 2048], replicated
- output 3: float32 [1, 2048, 512], replicated
- output 4: float32 [1, 512], replicated
- output 5: float32 [1, 2048, 512], replicated
All inputs are finite; a program needn't handle non-finite values.
Results may differ from a plain program's by a relative error of at most 0.00285763.
Values are sent between devices in bfloat16 or wider.
A program may use at most 1 GiB of HBM per device.

v0:
```python
import jax
import jax.numpy as jnp
from jax import lax
from jax.sharding import PartitionSpec as P

EPS = 1e-6


def rms_unit(values):
    return values * lax.rsqrt(jnp.mean(values * values, axis=-1, keepdims=True) + EPS)


def rms_back(values, grad_out):
    inv_rms = lax.rsqrt(jnp.mean(values * values, axis=-1, keepdims=True) + EPS)
    unit = values * inv_rms
    return inv_rms * (grad_out - unit * jnp.mean(grad_out * unit, axis=-1, keepdims=True))


def gelu_back(pre_act, grad_out):
    return jax.vjp(jax.nn.gelu, pre_act)[1](grad_out)[0]


def student_pass(student_in, targets, student_gain, student_up, student_down, grad_scale):
    n_feats = len(targets)
    state = student_in
    saved = []
    errors = []
    for feat_idx in range(n_feats):
        normed = rms_unit(state.astype(jnp.float32))
        act_in = (normed * student_gain[feat_idx]).astype(jnp.bfloat16)
        pre_act = jnp.einsum("bsd,df->bsf", act_in, student_up[feat_idx], preferred_element_type=jnp.float32)
        up_act = jax.nn.gelu(pre_act).astype(jnp.bfloat16)
        down_out = jnp.einsum("bsf,fd->bsd", up_act, student_down[feat_idx], preferred_element_type=jnp.float32)
        new_state = (state.astype(jnp.float32) + down_out).astype(jnp.bfloat16)
        errors.append(targets[feat_idx].astype(jnp.float32) - rms_unit(new_state.astype(jnp.float32)))
        saved.append((state, normed, act_in, pre_act, up_act, new_state))
        state = new_state
    loss_sum = sum(jnp.sum(error * error) for error in errors)
    d_res = jnp.zeros(student_in.shape, jnp.float32)
    grads_up = []
    grads_down = []
    grads_gain = []
    for feat_idx in reversed(range(n_feats)):
        state, normed, act_in, pre_act, up_act, new_state = saved[feat_idx]
        d_res = d_res + rms_back(new_state.astype(jnp.float32), -grad_scale * errors[feat_idx])
        d_out = d_res.astype(jnp.bfloat16)
        grads_down.append(jnp.einsum("bsf,bsd->fd", up_act, d_out, preferred_element_type=jnp.float32))
        d_up = jnp.einsum("bsd,fd->bsf", d_out, student_down[feat_idx], preferred_element_type=jnp.float32)
        d_pre = gelu_back(pre_act, d_up).astype(jnp.bfloat16)
        grads_up.append(jnp.einsum("bsd,bsf->df", act_in, d_pre, preferred_element_type=jnp.float32))
        d_act = jnp.einsum("bsf,df->bsd", d_pre, student_up[feat_idx], preferred_element_type=jnp.float32)
        grads_gain.append(jnp.sum(d_act * normed, axis=(0, 1)))
        if feat_idx > 0:
            d_res = d_res + rms_back(state.astype(jnp.float32), d_act * student_gain[feat_idx])
    return loss_sum, errors, jnp.stack(grads_up[::-1]), jnp.stack(grads_down[::-1]), jnp.stack(grads_gain[::-1])


def solution(mesh):
    dev_count = mesh.shape["data"] * mesh.shape["model"]
    all_axes = ("data", "model")

    def body(teacher_in, student_in, teacher_gain, teacher_up, teacher_down, student_gain, student_up, student_down, student_proj):
        n_feats = student_proj.shape[0]
        n_layers = teacher_up.shape[0]
        t_step = n_layers // n_feats
        seq_rows, seq_len, s_width = student_in.shape
        total = n_feats * seq_rows * dev_count * seq_len * s_width
        grad_scale = 2.0 / total
        hidden = teacher_in
        features = []
        targets = []
        for layer in range(n_layers):
            act_in = (rms_unit(hidden.astype(jnp.float32)) * teacher_gain[layer]).astype(jnp.bfloat16)
            act_full = lax.all_gather(act_in, "model", axis=1, tiled=True)
            pre_act = jnp.einsum("bsd,df->bsf", act_full, teacher_up[layer], preferred_element_type=jnp.float32)
            up_act = jax.nn.gelu(pre_act).astype(jnp.bfloat16)
            part_out = jnp.einsum("bsf,fd->bsd", up_act, teacher_down[layer], preferred_element_type=jnp.float32).astype(jnp.bfloat16)
            delta = lax.psum_scatter(part_out, "model", scatter_dimension=1, tiled=True)
            hidden = (hidden.astype(jnp.float32) + delta.astype(jnp.float32)).astype(jnp.bfloat16)
            if (layer + 1) % t_step == 0:
                local_target = jnp.einsum("bsd,de->bse", hidden, student_proj[layer // t_step], preferred_element_type=jnp.float32).astype(jnp.bfloat16)
                targets.append(lax.all_to_all(local_target, "model", 0, 1, tiled=True))
                features.append(hidden)
        loss_sum, errors, grad_up, grad_down, grad_gain = student_pass(student_in, targets, student_gain, student_up, student_down, grad_scale)
        proj_list = []
        for feat_idx in range(n_feats):
            error_back = lax.all_to_all(errors[feat_idx].astype(jnp.bfloat16), "model", 1, 0, tiled=True)
            proj_list.append(grad_scale * jnp.einsum("bsd,bse->de", features[feat_idx], error_back, preferred_element_type=jnp.float32))
        totals = lax.psum((loss_sum, grad_up, grad_down, grad_gain, jnp.stack(proj_list)), all_axes)
        return (totals[0] / total, totals[1], totals[2], totals[3], totals[4])

    return jax.shard_map(
        body,
        mesh=mesh,
        in_specs=(
            P("data", "model", None),
            P(("data", "model"), None, None),
            P(),
            P(None, None, "model"),
            P(None, "model", None),
            P(),
            P(),
            P(),
            P(),
        ),
        out_specs=(P(), P(), P(), P(), P()),
        check_vma=False,
    )
```

profile of v0, /device:TPU:1, one launch (start us, length us, event | category | flops | bytes accessed | tf_op | source)
XLA Modules:
  0.0 1347.9 jit_solution(8117585880461779773)
XLA Ops:
  7.2 0.0 copy-start
  7.2 0.0 copy-start.7
  7.2 0.0 all-gather.2.cloned.1.call-start
  7.2 7.2 fusion.19
  14.5 0.0 copy-done.7
  14.5 11.5 fusion.21
  26.0 0.0 all-gather.2.cloned.1.call-update
  26.1 0.0 reduce-scatter.2.cloned.1.call-start
  26.1 299.7 %all-gather.2.cloned.1.call-done = bf16[4,3072,2048]{2,1,0:T(8,128)(2,1)} async-done(((bf16[4,768,2048]{2,1,0:T(8,128)(2,1)}), bf16[4,3072,2048]{2,1,0:T(8,128)(2,1)}) %all-gather.2.cloned.1.call-update) | async-done | bytes 50331664 | tf_op jit(solution)/shard_map/all_gather | solution.py:74
  325.8 0.0 copy-start.8
  325.8 127.7 %fusion.6 = bf16[4,3072,2048]{2,1,0:T(8,128)(2,1)} fusion(bf16[4,3072,2048]{2,1,0:T(8,128)(2,1)} %all-gather.2.cloned.1.call-done, bf16[1,2048,2048]{2,1,0:T(8,128)(2,1)} %param.12), kind=kOutput, calls=%fused_computation.7 | convolution fusion | flops 103305707520 | bytes 109051904 | tf_op jit(solution)/shard_map/bsd,df->bsf/dot_general | solution.py:75
  453.6 0.0 copy-done.8
  453.6 111.0 %fusion.9 = bf16[4,3072,2048]{2,1,0:T(8,128)(2,1)} fusion(bf16[4,3072,2048]{2,1,0:T(8,128)(2,1)} %fusion.6, bf16[1,2048,2048]{2,1,0:T(8,128)(2,1)S(1)} %copy-done.8), kind=kOutput, calls=%fused_computation.10 | convolution fusion | flops 103104380928 | bytes 109051904 | tf_op jit(solution)/shard_map/bsf,fd->bsd/dot_general | solution.py:77
  564.6 0.0 reduce-scatter.2.cloned.1.call-update
  564.6 4.7 copy.24
  569.3 2.6 fusion.37
  571.8 0.0 copy-start.9
  571.8 323.9 %reduce-scatter.2.cloned.1.call-done = bf16[4,768,2048]{2,1,0:T(8,128)(2,1)} async-done(((bf16[4,3072,2048]{2,1,0:T(8,128)(2,1)}), bf16[4,768,2048]{2,1,0:T(8,128)(2,1)}) %reduce-scatter.2.cloned.1.call-update) | async-done | bytes 12582928 | tf_op jit(solution)/shard_map/reduce_scatter | solution.py:78
  895.7 17.9 %fusion.49 = bf16[4,768,512]{2,1,0:T(8,128)(2,1)} fusion(bf16[4,768,2048]{2,1,0:T(8,128)(2,1)} %param.9, bf16[4,768,2048]{2,1,0:T(8,128)(2,1)} %reduce-scatter.2.cloned.1.call-done, bf16[1,2048,512]{2,1,0:T(8,128)(2,1)} %param.17), kind=kOutput, calls=%fused_computation.60 | convolution fusion | flops 6469189632 | bytes 30408704 | tf_op jit(solution)/shard_map/bsd,de->bse/dot_general | solution.py:81
  913.6 5.9 all-to-all-start
  919.6 0.0 copy-done
  919.6 0.0 copy-done.9
  919.6 19.0 %multiply_convert_fusion = (bf16[3072,2048]{1,0:T(8,128)(2,1)}, f32[3072,2048]{1,0:T(8,128)}) fusion(bf16[1,512,2048]{2,1,0:T(8,128)(2,1)S(1)} %copy-done, bf16[1,3072,512]{1,2,0:T(8,128)(2,1)} %copy.24, f32[512]{0:T(512)S(1)} %bitcast.74, f32[3072]{0:T(1024)S(1)} %add_rsqrt_fusion.1), kind=kOutput, calls=%fused_computation.27 | convolution fusion | flops 6505365504 | bytes 43005952 | tf_op jit(solution)/shard_map/bsd,df->bsf/dot_general | solution.py:31
  938.6 14.2 %fusion.36 = (f32[3072]{0:T(1024)S(1)}, bf16[1,3072,512]{1,2,0:T(8,128)(2,1)}) fusion(bf16[3072,2048]{1,0:T(8,128)(2,1)} %get-tuple-element.14, bf16[1,2048,512]{2,1,0:T(8,128)(2,1)} %param.16, bf16[1,3072,512]{1,2,0:T(8,128)(2,1)} %copy.24), kind=kOutput, calls=%fused_computation.46 | convolution fusion | flops 6451885056 | bytes 20983808 | tf_op jit(solution)/shard_map/bsf,fd->bsd/dot_general | solution.py:33
  952.8 2.5 all-to-all-done
  955.3 5.4 bitcast_convert_fusion
  960.8 6.6 copy.25
  967.3 0.0 copy-start.1
  967.3 0.0 copy-start.3
  967.3 6.1 fusion.32
  973.5 0.0 copy-done.1
  973.5 0.3 copy-done.3
  973.8 3.6 fusion.48
  977.4 14.1 %copy.27 = bf16[1,3072,512]{2,0,1:T(2,128)(2,1)} copy(bf16[1,3072,512]{1,2,0:T(8,128)(2,1)} %get-tuple-element.12) | data formatting | bytes 6291456 | tf_op jit(solution)/shard_map/convert_element_type | solution.py:87
  991.4 0.5 broadcast.90
  992.0 22.1 %reduce.3 = bf16[3072,512]{1,0:T(8,128)(2,1)} reduce(bf16[3072,1,512]{2,1,0:T(2,128)(2,1)} %bitcast.69, bf16[]{:T(256)} %broadcast.90), dimensions={1}, to_apply=%bitcast.51.reduce_sub_computation | reduce | bytes 6291458
  1014.1 5.2 reshape.127
  1019.3 5.5 all-to-all-start.1
  1024.8 0.0 all-reduce.4.cloned.1.call-start
  1024.8 0.0 copy-start.2
  1024.8 28.3 %fusion.18 = bf16[3072,2048]{1,0:T(8,128)(2,1)} fusion(f32[3072,2048]{1,0:T(8,128)} %get-tuple-element.15, bf16[3072,512]{0,1:T(8,128)(2,1)} %get-tuple-element.13, bf16[1,2048,512]{2,1,0:T(8,128)(2,1)} %param.16), kind=kOutput, calls=%fused_computation.22 | convolution fusion | flops 6568280064 | bytes 42991616 | tf_op jit(solution)/shard_map/bsd,fd->bsf/dot_general | solution.py:48
  1053.1 0.0 copy-done.2
  1053.1 0.0 copy-start.6
  1053.1 11.2 convolution_bitcast_fusion.1
  1064.3 0.0 copy-done.6
  1064.3 11.3 convolution_bitcast_fusion
  1075.6 0.0 all-to-all-done.1
  1075.6 6.2 reshape.128
  1081.8 3.7 copy.31
  1085.5 14.8 %fusion.43 = f32[1,2048,512]{2,1,0:T(8,128)} fusion(bf16[4,768,512]{2,1,0:T(8,128)(2,1)S(1)} %bitcast.71, bf16[4,768,2048]{2,1,0:T(8,128)(2,1)} %param.9, bf16[4,768,2048]{2,1,0:T(8,128)(2,1)} %reduce-scatter.2.cloned.1.call-done), kind=kOutput, calls=%fused_computation.53 | convolution fusion | flops 6468665344 | bytes 32505856 | tf_op jit(solution)/shard_map/bsd,bse->de/dot_general | solution.py:88
  1100.2 0.0 all-reduce.4.cloned.1.call-update
  1100.3 10.6 fusion.31
  1110.8 41.7 %all-reduce = (f32[]{:T(128)}, f32[1,512]{1,0:T(1,128)}) all-reduce(f32[]{:T(128)} %get-tuple-element.6, f32[1,512]{1,0:T(1,128)S(1)} %bitcast.73), channel_id=1, replica_groups=mesh['data'=8,'model'=4] {'data','model'}, use_global_device_ids=true, to_apply=%region_5.0 | all-reduce | flops 513 | bytes 4104 | tf_op jit(solution)/shard_map/psum | solution.py:89
  1153.2 177.6 %all-reduce.4.cloned.1.call-done = (f32[1,512,2048]{2,1,0:T(8,128)}, f32[1,2048,512]{2,1,0:T(8,128)}, f32[1,2048,512]{2,1,0:T(8,128)}) async-done(((f32[1,512,2048]{2,1,0:T(8,128)}, f32[1,2048,512]{2,1,0:T(8,128)}, f32[1,2048,512]{2,1,0:T(8,128)}), (f32[1,512,2048]{2,1,0:T(8,128)}, f32[1,2048,512]{2,1,0:T(8,128)}, f32[1,2048,512]{2,1,0:T(8,128)})) %all-reduce.4.cloned.1.call-update) | async-done | bytes 12582928 | tf_op jit(solution)/shard_map/psum | solution.py:89
  1330.8 0.0 copy-start.5
  1330.8 0.0 copy-start.4
  1330.8 5.0 copy.35
  1335.8 0.0 copy-done.5
  1335.8 2.0 copy.36
  1337.8 0.0 copy-done.4
  1337.8 2.0 copy.37
  (4 shorter events, 0.0 us)
Async XLA Ops:
  7.2 912.4 %copy-start = (bf16[1,512,2048]{2,1,0:T(8,128)(2,1)S(1)}, bf16[1,512,2048]{2,1,0:T(8,128)(2,1)}, u32[]{:S(2)}) copy-start(bf16[1,512,2048]{2,1,0:T(8,128)(2,1)} %param.15) | copy-start | bytes 6291460
  7.2 7.3 copy-start.7
  7.2 318.7 %all-gather.2.cloned.1.call-start = ((), (), s32[]{:S(2)}) async-start(), calls=%async_computation.3 | async-start | bytes 62914560 | tf_op jit(solution)/shard_map/all_gather | solution.py:74
  26.1 869.7 %reduce-scatter.2.cloned.1.call-start = ((), (), s32[]{:S(2)}) async-start(), calls=%async_computation.4 | async-start | bytes 62914560 | tf_op jit(solution)/shard_map/reduce_scatter | solution.py:78
  325.8 127.7 %copy-start.8 = (bf16[1,2048,2048]{2,1,0:T(8,128)(2,1)S(1)}, bf16[1,2048,2048]{2,1,0:T(8,128)(2,1)}, u32[]{:S(2)}) copy-start(bf16[1,2048,2048]{2,1,0:T(8,128)(2,1)} %param.13) | copy-start | bytes 25165828
  571.8 347.7 %copy-start.9 = (f32[1,512]{1,0:T(1,128)S(1)}, f32[1,512]{1,0:T(1,128)}, u32[]{:S(2)}) copy-start(f32[1,512]{1,0:T(1,128)} %param.14) | copy-start | bytes 6148
  913.6 41.8 %all-to-all-start = ((bf16[4,768,512]{2,1,0:T(8,128)(2,1)}), bf16[4,768,512]{2,1,0:T(8,128)(2,1)}, u32[]{:S(2)}, u32[]{:S(2)}) async-start(bf16[4,768,512]{2,1,0:T(8,128)(2,1)} %fusion.49), calls=%async_computation.1 | async-start | bytes 6291456 | tf_op jit(solution)/shard_map/all_to_all | solution.py:82
  967.3 6.1 copy-start.1
  967.3 6.4 copy-start.3
  1019.3 56.3 %all-to-all-start.1 = ((bf16[4,2,196608]{2,1,0:T(2,128)(2,1)}), bf16[4,2,196608]{2,1,0:T(2,128)(2,1)}, u32[]{:S(2)}, u32[]{:S(2)}) async-start(bf16[4,2,196608]{2,1,0:T(2,128)(2,1)} %reshape.127), calls=%async_computation.2 | async-start | bytes 6291456 | tf_op jit(solution)/shard_map/all_to_all | solution.py:87
  1024.8 306.0 %all-reduce.4.cloned.1.call-start = ((), (), s32[]{:S(2)}) async-start(), calls=%async_computation.5 | async-start | bytes 25165824 | tf_op jit(solution)/shard_map/psum | solution.py:89
  1024.8 28.3 %copy-start.2 = (bf16[1,3072,512]{1,2,0:T(8,128)(2,1)S(1)}, bf16[1,3072,512]{1,2,0:T(8,128)(2,1)}, u32[]{:S(2)}) copy-start(bf16[1,3072,512]{1,2,0:T(8,128)(2,1)} %copy.24) | copy-start | bytes 9437188
  1053.1 11.2 copy-start.6
  1330.8 5.0 copy-start.5
  1330.8 7.0 copy-start.4
Sparse Core Ops, SparseCore 0:
  26.2 299.6 all-gather.1
  564.7 330.9 reduce-scatter.1
  1100.4 230.4 all-reduce.3
where the time goes:
time: 1360 us; the launch traced here: 1350 us
  waiting for transfers between devices  804 us (59%)
  matrix products  366 us (27%)
  other arithmetic  58.6 us (4%)
  local copies, waits for them, and re-layouts  50.2 us (4%)
  blocking collectives  41.7 us (3%)
  between operations  16 us (1%)
    reduce_scatter x1, waiting for transfers between devices, body(): delta = lax.psum_scatter(part_out, 'model', scatter_dimension=1, tiled=True)  324 us
    all_gather x1, waiting for transfers between devices, body(): act_full = lax.all_gather(act_in, 'model', axis=1, tiled=True)  300 us
    psum x1, waiting for transfers between devices, body(): lax.psum((loss_sum, grad_up, grad_down, grad_gain, jnp.stack(proj_list)),...  178 us
    dot_general x1, matrix products, body(): jnp.einsum('bsd,df->bsf', act_full, teacher_up[layer], preferred_element_...  128 us
    dot_general x1, matrix products, body(): jnp.einsum('bsf,fd->bsd', up_act, teacher_down[layer], preferred_element_...  111 us
    psum x1, blocking collectives, body(): lax.psum((loss_sum, grad_up, grad_down, grad_gain, jnp.stack(proj_list)),...  41.7 us
    unnamed x28, local copies, waits for them, and re-layouts  29.6 us
    dot_general x1, matrix products, student_pass(): jnp.einsum('bsd,fd->bsf', d_out, student_down[feat_idx], preferred_elemen...  28.3 us
  transfers between devices with their start and end apart: 5, of which 4 were waited for; matrix products, arithmetic and copies ran while one was open for 8% of the time, Pallas kernels for 0%

commit v1 on v0

v1 whole, which is shorter than its diff:
```python
import jax
import jax.numpy as jnp
from jax import lax
from jax.experimental import pallas as pl
from jax.experimental.pallas import tpu as pltpu
from jax.sharding import PartitionSpec as P

EPS = 1e-6
MESH = pl.DeviceIdType.MESH
F32 = jnp.float32
BF16 = jnp.bfloat16
GELU_K = 0.7978845608028654
GELU_C = 0.044715
TILE = 512
CHUNK = 512
PIECES = 8
X_STEPS = (10, 20, 30, 40, 50, 60, 66, 70)
VMEM_LIMIT = 67043328


def gelu(x):
    return 0.5 * x * (1.0 + jnp.tanh(GELU_K * (x + GELU_C * (x * x * x))))


def teacher_kernel(
    h_ref, gain_ref, w1_ref, w2_ref, s_ref,
    f_ref, w1g, w2g, sx_ref,
    act, acc, w1_v, w2_v, u_a, u_b, s_v,
    x_send, x_recv, y_send, y_recv, d_send, d_recv, g_send, g_recv, s_send, s_recv,
    w_sem, h_sem, f_sem, s_sem,
):
    data = lax.axis_index("data")
    model = lax.axis_index("model")
    y_par = lax.rem(data, 2)
    sib = (data, model + 1 - 2 * lax.rem(model, 2))
    x_nbr = (data, lax.rem(model + 2, 4))
    y_nbr = (data + 1 - 2 * y_par, model)
    rows, width = act.shape
    quarter = w1_ref.shape[1]
    half = quarter // 2
    piece = half // PIECES
    n_tiles = rows // TILE
    per_quarter = quarter // CHUNK
    n_chunks = 4 * per_quarter
    half_chunks = half // CHUNK
    per_chunk = CHUNK // piece

    def remote(src1, dst1, src2, dst2, send, recv, target):
        return (
            pltpu.make_async_remote_copy(src_ref=src1, dst_ref=dst1, send_sem=send.at[0], recv_sem=recv.at[0], device_id=target, device_id_type=MESH),
            pltpu.make_async_remote_copy(src_ref=src2, dst_ref=dst2, send_sem=send.at[1], recv_sem=recv.at[1], device_id=target, device_id_type=MESH),
        )

    def cols(start, size):
        return pl.ds(pl.multiple_of(start, size), size)

    def x_copy(p):
        where = cols(y_par * half + p * piece, piece)
        return remote(w1_ref.at[:, where], w1g.at[1, :, where], w2_ref.at[where], w2g.at[1, where], x_send.at[p], x_recv.at[p], x_nbr)

    def y_copy(p, mine):
        where = cols((y_par if mine else 1 - y_par) * half + p * piece, piece)
        return remote(w1g.at[1, :, where], w1g.at[1, :, where], w2g.at[1, where], w2g.at[1, where], y_send.at[p], y_recv.at[p], y_nbr)

    def d_copy(i):
        where = cols(i * CHUNK, CHUNK)
        return remote(w1_ref.at[:, where], w1g.at[0, :, where], w2_ref.at[where], w2g.at[0, where], d_send.at[i], d_recv.at[i], sib)

    def far_cols(group):
        side = y_par if group % 2 == 0 else 1 - y_par
        return cols(side * half + (group // 2) * CHUNK, CHUNK)

    def g_copy(group):
        where = far_cols(group)
        return remote(w1g.at[1, :, where], w1g.at[2, :, where], w2g.at[1, where], w2g.at[2, where], g_send.at[group], g_recv.at[group], sib)

    def s_copy(k):
        other = lax.rem(model + k, 4)
        return pltpu.make_async_remote_copy(
            src_ref=s_ref.at[other], dst_ref=sx_ref.at[model], send_sem=s_send.at[k - 1], recv_sem=s_recv.at[k - 1],
            device_id=(data, other), device_id_type=MESH,
        )

    def s_arrival(k):
        other = lax.rem(model + 4 - k, 4)
        return pltpu.make_async_remote_copy(
            src_ref=s_ref.at[other], dst_ref=sx_ref.at[other], send_sem=s_send.at[k - 1], recv_sem=s_recv.at[k - 1],
            device_id=(data, other), device_id_type=MESH,
        )

    def load(src1, src2, slot):
        pltpu.make_async_copy(src1, w1_v.at[slot], w_sem.at[slot, 0]).start()
        pltpu.make_async_copy(src2, w2_v.at[slot], w_sem.at[slot, 1]).start()

    def load_wait(slot):
        pltpu.make_async_copy(w1_ref.at[:, pl.ds(0, CHUNK)], w1_v.at[slot], w_sem.at[slot, 0]).wait()
        pltpu.make_async_copy(w2_ref.at[pl.ds(0, CHUNK)], w2_v.at[slot], w_sem.at[slot, 1]).wait()

    def tile_rows(t):
        return pl.ds(pl.multiple_of(t * TILE, TILE), TILE)

    def h_load(t):
        return pltpu.make_async_copy(h_ref.at[tile_rows(t)], act.at[tile_rows(t)], h_sem.at[t])

    def f_store(t):
        return pltpu.make_async_copy(act.at[tile_rows(t)], f_ref.at[tile_rows(t)], f_sem.at[t])

    for t in range(n_tiles):
        h_load(t).start()
    load(w1_ref.at[:, pl.ds(0, CHUNK)], w2_ref.at[pl.ds(0, CHUNK)], 0)
    own_in = pltpu.make_async_copy(s_ref.at[model], s_v, s_sem.at[0])
    own_in.start()

    barrier = pltpu.get_barrier_semaphore()
    others = [(data, lax.rem(model + k, 4)) for k in (1, 2, 3)] + [y_nbr]
    for other in others:
        pl.semaphore_signal(barrier, inc=1, device_id=other, device_id_type=MESH)
    pl.semaphore_wait(barrier, len(others))

    for p in range(2):
        for copy in x_copy(p):
            copy.start()
    for i in range(per_quarter):
        for copy in d_copy(i):
            copy.start()

    u_b[...] = jnp.zeros_like(u_b)
    sub = 32

    @pl.loop(0, n_tiles)
    def _(t):
        h_load(t).wait()

        @pl.loop(0, TILE // sub)
        def _(k):
            where = pl.ds(pl.multiple_of(t * TILE + k * sub, sub), sub)
            values = act[where, :].astype(F32)
            inv = lax.rsqrt(jnp.mean(values * values, axis=-1, keepdims=True) + EPS)
            act[where, :] = ((values * inv) * gain_ref[...]).astype(BF16)
            acc[where, :] = jnp.zeros((sub, width), F32)

    own_in.wait()
    own_out = pltpu.make_async_copy(s_v, sx_ref.at[model], s_sem.at[1])
    own_out.start()

    pairs = n_tiles // 2

    @pl.loop(0, n_chunks * pairs)
    def _(i):
        c = i // pairs
        j = lax.rem(i, pairs)
        slot = lax.rem(c, 2)
        first = 2 * j
        before = lax.rem(first + n_tiles - 1, n_tiles)
        slot_before = jnp.where((j == 0) & (c > 0), 1 - slot, slot)

        for p, step in enumerate(X_STEPS):

            @pl.when(2 * i == step)
            def _(p=p):
                for copy in x_copy(p):
                    copy.wait_recv()
                for copy in y_copy(p, True):
                    copy.start()
                if p + 2 < PIECES:
                    for copy in x_copy(p + 2):
                        copy.start()
                if p == PIECES - 2:
                    for k in (1, 2, 3):
                        s_copy(k).start()
                if p % per_chunk == per_chunk - 1:
                    for copy in g_copy(2 * (p // per_chunk)):
                        copy.start()

        @pl.when((j == 0))
        def _():
            load_wait(slot)

        coming = c + 1
        loads = j == pairs - 1

        @pl.when(loads & (coming < per_quarter))
        def _():
            where = cols(coming * CHUNK, CHUNK)
            load(w1_ref.at[:, where], w2_ref.at[where], 1 - slot)

        for k in range(per_quarter):

            @pl.when(loads & (coming == per_quarter + k))
            def _(k=k):
                for copy in d_copy(k):
                    copy.wait_recv()
                where = cols(k * CHUNK, CHUNK)
                load(w1g.at[0, :, where], w2g.at[0, where], 1 - slot)

        for group in range(per_quarter):
            place = 2 * per_quarter + 2 * group

            @pl.when(loads & (coming == place))
            def _(group=group):
                if group % 2 == 1:
                    for q in range(per_chunk):
                        for copy in y_copy((group // 2) * per_chunk + q, False):
                            copy.wait_recv()
                    for copy in g_copy(group):
                        copy.start()
                where = far_cols(group)
                load(w1g.at[1, :, where], w2g.at[1, where], 1 - slot)

            @pl.when(loads & (coming == place + 1))
            def _(group=group):
                for copy in g_copy(group):
                    copy.wait_recv()
                where = far_cols(group)
                load(w1g.at[2, :, where], w2g.at[2, where], 1 - slot)

        @pl.when((c == n_chunks - 1) & (j > 0))
        def _():
            h_load(first - 2).start()
            h_load(first - 1).start()

        u_a[...] = gelu(jnp.dot(act[tile_rows(first), :], w1_v[slot], preferred_element_type=F32)).astype(BF16)
        acc[tile_rows(before), :] += jnp.dot(u_b[...], w2_v[slot_before], preferred_element_type=F32)
        u_b[...] = gelu(jnp.dot(act[tile_rows(first + 1), :], w1_v[slot], preferred_element_type=F32)).astype(BF16)
        acc[tile_rows(first), :] += jnp.dot(u_a[...], w2_v[slot], preferred_element_type=F32)

    h_load(n_tiles - 2).start()
    h_load(n_tiles - 1).start()
    acc[pl.ds((n_tiles - 1) * TILE, TILE), :] += jnp.dot(u_b[...], w2_v[(n_chunks - 1) % 2], preferred_element_type=F32)

    @pl.loop(0, n_tiles)
    def _(t):
        h_load(t).wait()

        @pl.loop(0, TILE // sub)
        def _(k):
            where = pl.ds(pl.multiple_of(t * TILE + k * sub, sub), sub)
            delta = acc[where, :].astype(BF16).astype(F32)
            act[where, :] = (act[where, :].astype(F32) + delta).astype(BF16)

        f_store(t).start()

    for k in (1, 2, 3):
        s_arrival(k).wait_recv()
        s_copy(k).wait_send()
    own_out.wait()
    for p in range(PIECES):
        for copy in x_copy(p) + y_copy(p, True):
            copy.wait_send()
    for i in range(per_quarter):
        for copy in d_copy(i) + g_copy(i):
            copy.wait_send()
    for t in range(n_tiles):
        f_store(t).wait()


def teacher_layer(hidden, gain, w_up, w_down, student_rows):
    rows, width = hidden.shape
    quarter = w_up.shape[1]
    per_quarter = quarter // CHUNK
    n_tiles = rows // TILE
    dma = pltpu.SemaphoreType.DMA
    anywhere = pl.BlockSpec(memory_space=pl.ANY)
    return pl.pallas_call(
        teacher_kernel,
        out_shape=(
            jax.ShapeDtypeStruct((rows, width), BF16),
            jax.ShapeDtypeStruct((3, width, quarter), BF16),
            jax.ShapeDtypeStruct((3, quarter, width), BF16),
            jax.ShapeDtypeStruct(student_rows.shape, BF16),
        ),
        in_specs=[anywhere, pl.BlockSpec(memory_space=pltpu.VMEM), anywhere, anywhere, anywhere],
        out_specs=(anywhere,) * 4,
        scratch_shapes=[
            pltpu.VMEM((rows, width), BF16),
            pltpu.VMEM((rows, width), F32),
            pltpu.VMEM((2, width, CHUNK), BF16),
            pltpu.VMEM((2, CHUNK, width), BF16),
            pltpu.VMEM((TILE, CHUNK), BF16),
            pltpu.VMEM((TILE, CHUNK), BF16),
            pltpu.VMEM(student_rows.shape[1:], BF16),
            dma((PIECES, 2)), dma((PIECES, 2)), dma((PIECES, 2)), dma((PIECES, 2)),
            dma((per_quarter, 2)), dma((per_quarter, 2)), dma((per_quarter, 2)), dma((per_quarter, 2)),
            dma((3,)), dma((3,)),
            dma((2, 2)), dma((n_tiles,)), dma((n_tiles,)), dma((2,)),
        ],
        compiler_params=pltpu.CompilerParams(collective_id=0, has_side_effects=True, vmem_limit_bytes=VMEM_LIMIT),
        cost_estimate=pl.CostEstimate(flops=16 * rows * width * quarter, bytes_accessed=8 * width * quarter * 2, transcendentals=0),
        name="teacher",
    )(hidden, gain, w_up, w_down, student_rows)


def nt_dot(a, b):
    return lax.dot_general(a, b, (((1,), (1,)), ((), ())), preferred_element_type=F32)


def tn_dot(a, b):
    return lax.dot_general(a, b, (((0,), (0,)), ((), ())), preferred_element_type=F32)


def student_kernel(scale_ref, f_ref, s_ref, gain_ref, up_ref, down_ref, proj_ref, g_ref, pre, err_t):
    i = pl.program_id(0)
    width = s_ref.shape[1]
    scale = scale_ref[0]

    @pl.when(i == 0)
    def _():
        g_ref[...] = jnp.zeros_like(g_ref)

    state = s_ref[...].astype(F32)
    normed = state * lax.rsqrt(jnp.mean(state * state, axis=-1, keepdims=True) + EPS)
    act_in = (normed * gain_ref[...]).astype(BF16)
    pre[...] = jnp.dot(act_in, up_ref[...], preferred_element_type=F32)
    up_act = gelu(pre[...]).astype(BF16)
    new_state = (state + jnp.dot(up_act, down_ref[...], preferred_element_type=F32)).astype(BF16).astype(F32)
    target = jnp.dot(f_ref[...], proj_ref[...], preferred_element_type=F32).astype(BF16).astype(F32)
    inv = lax.rsqrt(jnp.mean(new_state * new_state, axis=-1, keepdims=True) + EPS)
    unit = new_state * inv
    error = target - unit
    grad = -scale * error
    d_res = inv * (grad - unit * jnp.mean(grad * unit, axis=-1, keepdims=True))
    d_out = d_res.astype(BF16)
    g_ref[pl.ds(2 * width, width), :] += scale * tn_dot(error.astype(BF16), f_ref[...])
    g_ref[pl.ds(width, width), :] += tn_dot(d_out, up_act)
    d_up = nt_dot(d_out, down_ref[...])
    x = pre[...]
    x2 = x * x
    th = jnp.tanh(GELU_K * (x + GELU_C * (x2 * x)))
    slope = 0.5 * (1.0 + th) + 0.5 * x * (1.0 - th * th) * (GELU_K * (1.0 + 3.0 * GELU_C * x2))
    d_pre = (slope * d_up).astype(BF16)
    g_ref[pl.ds(0, width), :] += tn_dot(act_in, d_pre)
    d_act = nt_dot(d_pre, up_ref[...])
    g_ref[pl.ds(3 * width, 1), pl.ds(0, width)] += jnp.sum(d_act * normed, axis=0, keepdims=True)
    squares = jnp.sum(error * error, axis=0, keepdims=True)
    g_ref[pl.ds(3 * width, 1), pl.ds(width, width)] += squares


def student_layer(scale, feature, student_rows, gain, w_up, w_down, proj):
    rows, t_width = feature.shape
    width = student_rows.shape[1]
    wide = w_up.shape[1]
    tile = 512
    whole = pl.BlockSpec(memory_space=pltpu.VMEM)
    return pl.pallas_call(
        student_kernel,
        out_shape=jax.ShapeDtypeStruct((3 * width + 8, wide), F32),
        grid=(rows // tile,),
        in_specs=[
            pl.BlockSpec(memory_space=pltpu.SMEM),
            pl.BlockSpec((tile, t_width), lambda i: (i, 0)),
            pl.BlockSpec((tile, width), lambda i: (i, 0)),
            whole, whole, whole, whole,
        ],
        out_specs=pl.BlockSpec(memory_space=pltpu.VMEM),
        scratch_shapes=[pltpu.VMEM((tile, wide), F32), pltpu.VMEM((8, 128), F32)],
        compiler_params=pltpu.CompilerParams(dimension_semantics=("arbitrary",), vmem_limit_bytes=VMEM_LIMIT),
        cost_estimate=pl.CostEstimate(flops=12 * rows * width * wide + 4 * rows * width * t_width, bytes_accessed=2 * rows * (t_width + width), transcendentals=0),
        name="student",
    )(scale, feature, student_rows, gain, w_up, w_down, proj)


def solution(mesh):
    dev_count = mesh.shape["data"] * mesh.shape["model"]
    all_axes = ("data", "model")

    def body(teacher_in, student_in, teacher_gain, teacher_up, teacher_down, student_gain, student_up, student_down, student_proj):
        seqs, tokens, t_width = teacher_in.shape
        seq_rows, seq_len, width = student_in.shape
        total = seq_rows * dev_count * seq_len * width
        grad_scale = 2.0 / total
        feature, _, _, rows = teacher_layer(
            teacher_in.reshape(seqs * tokens, t_width), teacher_gain, teacher_up[0], teacher_down[0],
            student_in.reshape(seqs, tokens, width),
        )
        sums = student_layer(
            jnp.full((1,), grad_scale, F32), feature, rows.reshape(seqs * tokens, width),
            student_gain, student_up[0], student_down[0], student_proj[0],
        )
        sums = lax.psum(sums, all_axes)
        grad_up = sums[None, :width]
        grad_down = sums[width : 2 * width].T[None]
        grad_proj = sums[2 * width : 3 * width].T[None]
        grad_gain = sums[None, 3 * width, :width]
        loss = jnp.sum(sums[3 * width, width : 2 * width]) / total
        return (loss, grad_up, grad_down, grad_gain, grad_proj)

    return jax.shard_map(
        body,
        mesh=mesh,
        in_specs=(
            P("data", "model", None),
            P(("data", "model"), None, None),
            P(),
            P(None, None, "model"),
            P(None, "model", None),
            P(),
            P(),
            P(),
            P(),
        ),
        out_specs=(P(), P(), P(), P(), P()),
        check_vma=False,
    )
```

time: 1360 us -> 623 us (0.46)
  waiting for transfers between devices: 804 us -> 232 us
  matrix products: 366 us -> 0 us
  Pallas kernels: 0 us -> 351 us
  other arithmetic: 58.6 us -> 1.91 us
  blocking collectives: 41.7 us -> 0 us
  local copies, waits for them, and re-layouts: 50.2 us -> 20.5 us
    dot_general x10 -> x0, matrix products: 366 us -> none  [the longest x1 128 us: body(): jnp.einsum('bsd,df->bsf', act_full, teacher_up[layer], preferred_element_...]
    pallas_call x0 -> x2, Pallas kernels: none -> 351 us  [the longest x1 282 us: teacher_layer(): pl.pallas_call(teacher_kernel, out_shape=(jax.ShapeDtypeStruct((rows, wid...]
    reduce_scatter x1 -> x0, waiting for transfers between devices: 324 us -> none  [body(): delta = lax.psum_scatter(part_out, 'model', scatter_dimension=1, tiled=True)]
    all_gather x1 -> x0, waiting for transfers between devices: 300 us -> none  [body(): act_full = lax.all_gather(act_in, 'model', axis=1, tiled=True)]
    psum x1, waiting for transfers between devices: 178 us -> 232 us  [body(): sums = lax.psum(sums, all_axes)]
    psum x1 -> x0, blocking collectives: 41.7 us -> none  [body(): lax.psum((loss_sum, grad_up, grad_down, grad_gain, jnp.stack(proj_list)),...]
    unnamed x1 -> x0, other arithmetic: 22.1 us -> none
    convert_element_type x2 -> x0, local copies, waits for them, and re-layouts: 20.6 us -> none  [the longest x1 14.1 us: body(): errors[feat_idx].astype(jnp.bfloat16)]
  transfers between devices with their start and end apart: 5 -> 1, of which waited for: 4 -> 1; matrix products, arithmetic and copies ran while one was open for 8% -> 0% of each run, Pallas kernels for 0% -> 0%
where the time goes in v1:
time: 623 us; the launch traced here: 621 us
  Pallas kernels  351 us (56%)
  waiting for transfers between devices  232 us (37%)
  local copies, waits for them, and re-layouts  20.5 us (3%)
  between operations  15.8 us (3%)
    pallas_call x1, Pallas kernels, teacher_layer(): pl.pallas_call(teacher_kernel, out_shape=(jax.ShapeDtypeStruct((rows, wid...  282 us
    psum x1, waiting for transfers between devices, body(): sums = lax.psum(sums, all_axes)  232 us
    pallas_call x1, Pallas kernels, student_layer(): pl.pallas_call(student_kernel, out_shape=jax.ShapeDtypeStruct((3 * width...  68.7 us
  transfers between devices with their start and end apart: 1, of which 1 were waited for; matrix products, arithmetic and copies ran while one was open for 0% of the time, Pallas kernels for 0%

profile of v1, /device:TPU:1, one launch (start us, length us, event | category | flops | bytes accessed | tf_op | source)
XLA Modules:
  0.0 621.3 jit_solution(12408749574873451296)
XLA Ops:
  7.2 0.0 all-reduce.2.cloned.1.call-start
  7.2 282.2 %teacher.1 = (bf16[3072,2048]{1,0:T(8,128)(2,1)}, bf16[3,2048,2048]{2,1,0:T(8,128)(2,1)}, bf16[3,2048,2048]{2,1,0:T(8,128)(2,1)}, bf16[4,768,512]{2,1,0:T(8,128)(2,1)}) custom-call(bf16[3072,2048]{1,0:T(8,128)(2,1)} %bitcast.18, f32[1,2048]{1,0:T(1,128)} %gain_ref.2, bf16[2048,2048]{1,0:T(8,128)(2,1)} %bitcast.19, bf16[2048,2048]{1,0:T(8,128)(2,1)} %bitcast.20, ...), custom_call_target="tpu_custom_call" | custom-call | flops 206158430208 | bytes 67108864 | tf_op jit(solution)/shard_map/teacher/pallas_call | solution.py:264
  289.4 68.7 %student.1 = f32[1544,2048]{1,0:T(8,128)} custom-call(f32[1]{0:T(128)} %constant.1.clone.1.scale_ref, bf16[3072,2048]{1,0:T(8,128)(2,1)} %get-tuple-element.7.f_ref, bf16[3072,512]{1,0:T(8,128)(2,1)} %bitcast.25, f32[1,512]{1,0:T(1,128)} %gain_ref.3, bf16[512,2048]{1,0:T(8,128)(2,1)} %bitcast.22, bf16[2048,512]{1,0:T(8,128)(2,1)} %bitcast.23, ...), custom_call_target="tpu_custom_call" | custom-call | flops 51539607552 | bytes 15728640 | tf_op jit(solution)/shard_map/student/pallas_call | solution.py:344
  358.1 0.0 all-reduce.2.cloned.1.call-update
  358.1 232.1 %all-reduce.2.cloned.1.call-done = f32[1544,2048]{1,0:T(8,128)} async-done(((f32[1544,2048]{1,0:T(8,128)}), f32[1544,2048]{1,0:T(8,128)}) %all-reduce.2.cloned.1.call-update) | async-done | bytes 12648464 | tf_op jit(solution)/shard_map/psum | solution.py:379
  590.2 9.8 %slice_bitcast_fusion = (f32[1,2048,512]{1,2,0:T(8,128)}, f32[1,2048,512]{1,2,0:T(8,128)}, f32[1,512,2048]{2,1,0:T(8,128)}) fusion(f32[1544,2048]{1,0:T(8,128)} %all-reduce.2.cloned.1.call-done), kind=kLoop, calls=%fused_computation | loop fusion | bytes 25165824 | tf_op jit(solution)/shard_map/broadcast_in_dim | solution.py:382
  600.0 5.3 copy.15
  605.4 5.3 copy.14
  610.7 1.9 fusion
Async XLA Ops:
  7.2 583.1 %all-reduce.2.cloned.1.call-start = ((), (), s32[]{:S(2)}) async-start(), calls=%async_computation | async-start | bytes 25296896 | tf_op jit(solution)/shard_map/psum | solution.py:379
Sparse Core Ops, SparseCore 0:
  358.2 231.9 all-reduce.1

commit v2 on v1

--- a/solution.py
+++ b/solution.py
@@ -298,7 +298,7 @@
     return lax.dot_general(a, b, (((0,), (0,)), ((), ())), preferred_element_type=F32)
 
 
-def student_kernel(scale_ref, f_ref, s_ref, gain_ref, up_ref, down_ref, proj_ref, g_ref, pre, err_t):
+def student_kernel(scale_ref, f_ref, s_ref, gain_ref, up_ref, down_ref, proj_ref, g_ref, small_ref, pre):
     i = pl.program_id(0)
     width = s_ref.shape[1]
     scale = scale_ref[0]
@@ -306,6 +306,7 @@
     @pl.when(i == 0)
     def _():
         g_ref[...] = jnp.zeros_like(g_ref)
+        small_ref[...] = jnp.zeros_like(small_ref)
 
     state = s_ref[...].astype(F32)
     normed = state * lax.rsqrt(jnp.mean(state * state, axis=-1, keepdims=True) + EPS)
@@ -330,9 +331,9 @@
     d_pre = (slope * d_up).astype(BF16)
     g_ref[pl.ds(0, width), :] += tn_dot(act_in, d_pre)
     d_act = nt_dot(d_pre, up_ref[...])
-    g_ref[pl.ds(3 * width, 1), pl.ds(0, width)] += jnp.sum(d_act * normed, axis=0, keepdims=True)
+    small_ref[pl.ds(0, 1), :] += jnp.sum(d_act * normed, axis=0, keepdims=True)
     squares = jnp.sum(error * error, axis=0, keepdims=True)
-    g_ref[pl.ds(3 * width, 1), pl.ds(width, width)] += squares
+    small_ref[pl.ds(1, 1), :] += squares
 
 
 def student_layer(scale, feature, student_rows, gain, w_up, w_down, proj):
@@ -343,7 +344,7 @@
     whole = pl.BlockSpec(memory_space=pltpu.VMEM)
     return pl.pallas_call(
         student_kernel,
-        out_shape=jax.ShapeDtypeStruct((3 * width + 8, wide), F32),
+        out_shape=(jax.ShapeDtypeStruct((3 * width, wide), F32), jax.ShapeDtypeStruct((8, width), F32)),
         grid=(rows // tile,),
         in_specs=[
             pl.BlockSpec(memory_space=pltpu.SMEM),
@@ -351,17 +352,177 @@
             pl.BlockSpec((tile, width), lambda i: (i, 0)),
             whole, whole, whole, whole,
         ],
-        out_specs=pl.BlockSpec(memory_space=pltpu.VMEM),
-        scratch_shapes=[pltpu.VMEM((tile, wide), F32), pltpu.VMEM((8, 128), F32)],
+        out_specs=(pl.BlockSpec(memory_space=pltpu.VMEM),) * 2,
+        scratch_shapes=[pltpu.VMEM((tile, wide), F32)],
         compiler_params=pltpu.CompilerParams(dimension_semantics=("arbitrary",), vmem_limit_bytes=VMEM_LIMIT),
         cost_estimate=pl.CostEstimate(flops=12 * rows * width * wide + 4 * rows * width * t_width, bytes_accessed=2 * rows * (t_width + width), transcendentals=0),
         name="student",
     )(scale, feature, student_rows, gain, w_up, w_down, proj)
 
 
+def total_kernel(
+    g_ref, small_ref, out_ref, small_out,
+    work, inbox, whole, small_v, small_in,
+    rs_send, rs_recv, ag_send, ag_recv, sm_send, sm_recv, in_sem, out_sem,
+):
+    data = lax.axis_index("data")
+    model = lax.axis_index("model")
+    bits = {
+        "core": lax.rem(model, 2),
+        "x": model // 2,
+        "y": lax.rem(data, 2),
+        "z": lax.rem(data // 2, 2),
+        "zz": data // 4,
+    }
+    turn = {name: 1 - 2 * bit for name, bit in bits.items()}
+    partner = {
+        "core": (data, model + turn["core"]),
+        "x": (data, model + 2 * turn["x"]),
+        "y": (data + turn["y"], model),
+        "z": (data + 2 * turn["z"], model),
+        "zz": (data + 4 * turn["zz"], model),
+    }
+    orders = (("core", "x", "y", "z", "zz"), ("core", "y", "z", "x", "zz"), ("core", "z", "x", "y", "zz"))
+    stages = len(orders[0])
+    parts = len(orders)
+    height = work.shape[0] // parts
+    sizes = [height >> (k + 1) for k in range(stages)]
+    slots = [height - (height >> k) for k in range(stages)]
+
+    def block(start, size):
+        return pl.ds(pl.multiple_of(start, size), size)
+
+    for part in range(parts):
+        pltpu.make_async_copy(g_ref.at[pl.ds(part * height, height)], work.at[pl.ds(part * height, height)], in_sem.at[part]).start()
+
+    barrier = pltpu.get_barrier_semaphore()
+    for target in partner.values():
+        pl.semaphore_signal(barrier, inc=1, device_id=target, device_id_type=MESH)
+    pl.semaphore_wait(barrier, stages)
+
+    bases = [[part * height] for part in range(parts)]
+    for part in range(parts):
+        for k in range(stages):
+            bases[part].append(bases[part][k] + bits[orders[part][k]] * sizes[k])
+
+    def rs_copy(part, k):
+        name = orders[part][k]
+        gone = block(bases[part][k] + (1 - bits[name]) * sizes[k], sizes[k])
+        return pltpu.make_async_remote_copy(
+            src_ref=work.at[gone], dst_ref=inbox.at[pl.ds(part * height + slots[k], sizes[k])],
+            send_sem=rs_send.at[part, k], recv_sem=rs_recv.at[part, k], device_id=partner[name], device_id_type=MESH,
+        )
+
+    def ag_copy(part, k, mine):
+        name = orders[part][k]
+        start = bases[part][k] + (bits[name] if mine else 1 - bits[name]) * sizes[k]
+        where = block(start, sizes[k])
+        return pltpu.make_async_remote_copy(
+            src_ref=whole.at[where], dst_ref=whole.at[where],
+            send_sem=ag_send.at[part, k], recv_sem=ag_recv.at[part, k], device_id=partner[name], device_id_type=MESH,
+        )
+
+    def sm_copy(k):
+        return pltpu.make_async_remote_copy(
+            src_ref=small_v.at[k], dst_ref=small_in.at[k],
+            send_sem=sm_send.at[k], recv_sem=sm_recv.at[k], device_id=partner[orders[0][k]], device_id_type=MESH,
+        )
+
+    small_v[0] = small_ref[...]
+    for part in range(parts):
+        pltpu.make_async_copy(g_ref.at[pl.ds(part * height, height)], work.at[pl.ds(part * height, height)], in_sem.at[part]).wait()
+        rs_copy(part, 0).start()
+    sm_copy(0).start()
+    strip = 16
+    for k in range(stages):
+        for part in range(parts):
+            rs_copy(part, k).wait_recv()
+            into = whole if k == stages - 1 else work
+
+            @pl.loop(0, sizes[k] // strip)
+            def _(i, k=k, part=part, into=into):
+                kept = pl.ds(pl.multiple_of(bases[part][k + 1] + i * strip, strip), strip)
+                came = pl.ds(pl.multiple_of(part * height + slots[k] + i * strip, strip), strip)
+                into[kept, :] = work[kept, :] + inbox[came, :]
+
+            if k + 1 < stages:
+                rs_copy(part, k + 1).start()
+            else:
+                ag_copy(part, k, True).start()
+        sm_copy(k).wait_recv()
+        if k + 1 < stages:
+            small_v[k + 1] = small_v[k] + small_in[k]
+            sm_copy(k + 1).start()
+        else:
+            small_out[...] = small_v[k] + small_in[k]
+
+    for k in reversed(range(stages)):
+        for part in range(parts):
+            ag_copy(part, k, False).wait_recv()
+            if k > 0:
+                ag_copy(part, k - 1, True).start()
+            else:
+                pltpu.make_async_copy(whole.at[pl.ds(part * height, height)], out_ref.at[pl.ds(part * height, height)], out_sem.at[part]).start()
+
+    for k in range(stages):
+        for part in range(parts):
+            rs_copy(part, k).wait_send()
+            ag_copy(part, k, True).wait_send()
+        sm_copy(k).wait_send()
+    for part in range(parts):
+        pltpu.make_async_copy(whole.at[pl.ds(part * height, height)], out_ref.at[pl.ds(part * height, height)], out_sem.at[part]).wait()
+
+
+def total_over_devices(sums, small):
+    rows, width = sums.shape
+    dma = pltpu.SemaphoreType.DMA
+    anywhere = pl.BlockSpec(memory_space=pl.ANY)
+    vmem = pl.BlockSpec(memory_space=pltpu.VMEM)
+    return pl.pallas_call(
+        total_kernel,
+        out_shape=(jax.ShapeDtypeStruct(sums.shape, F32), jax.ShapeDtypeStruct(small.shape, F32)),
+        in_specs=[anywhere, vmem],
+        out_specs=(anywhere, vmem),
+        scratch_shapes=[
+            pltpu.VMEM((rows, width), F32),
+            pltpu.VMEM((rows, width), F32),
+            pltpu.VMEM((rows, width), F32),
+            pltpu.VMEM((5,) + small.shape, F32),
+            pltpu.VMEM((5,) + small.shape, F32),
+            dma((3, 5)), dma((3, 5)), dma((3, 5)), dma((3, 5)), dma((5,)), dma((5,)), dma((3,)), dma((3,)),
+        ],
+        compiler_params=pltpu.CompilerParams(collective_id=1, has_side_effects=True, vmem_limit_bytes=VMEM_LIMIT),
+        name="total",
+    )(sums, small)
+
+
+def finish_kernel(up_ref, down_ref, proj_ref, up_out, down_out, proj_out):
+    up_out[...] = up_ref[...]
+    down_out[...] = down_ref[...].T
+    proj_out[...] = proj_ref[...].T
+
+
+def finish(sums):
+    height = sums.shape[0] // 3
+    wide = sums.shape[1]
+    step = 512
+    flat = jax.ShapeDtypeStruct((height, wide), F32)
+    tall = jax.ShapeDtypeStruct((wide, height), F32)
+    across = pl.BlockSpec((height, step), lambda i: (0, i))
+    along = pl.BlockSpec((step, height), lambda i: (i, 0))
+    return pl.pallas_call(
+        finish_kernel,
+        out_shape=(flat, tall, tall),
+        grid=(wide // step,),
+        in_specs=[pl.BlockSpec((height, step), lambda i, part=part: (part, i)) for part in range(3)],
+        out_specs=(across, along, along),
+        compiler_params=pltpu.CompilerParams(dimension_semantics=("arbitrary",), vmem_limit_bytes=VMEM_LIMIT),
+        name="finish",
+    )(sums, sums, sums)
+
+
 def solution(mesh):
     dev_count = mesh.shape["data"] * mesh.shape["model"]
-    all_axes = ("data", "model")
 
     def body(teacher_in, student_in, teacher_gain, teacher_up, teacher_down, student_gain, student_up, student_down, student_proj):
         seqs, tokens, t_width = teacher_in.shape
@@ -372,17 +533,14 @@
             teacher_in.reshape(seqs * tokens, t_width), teacher_gain, teacher_up[0], teacher_down[0],
             student_in.reshape(seqs, tokens, width),
         )
-        sums = student_layer(
+        sums, small = student_layer(
             jnp.full((1,), grad_scale, F32), feature, rows.reshape(seqs * tokens, width),
             student_gain, student_up[0], student_down[0], student_proj[0],
         )
-        sums = lax.psum(sums, all_axes)
-        grad_up = sums[None, :width]
-        grad_down = sums[width : 2 * width].T[None]
-        grad_proj = sums[2 * width : 3 * width].T[None]
-        grad_gain = sums[None, 3 * width, :width]
-        loss = jnp.sum(sums[3 * width, width : 2 * width]) / total
-        return (loss, grad_up, grad_down, grad_gain, grad_proj)
+        sums, small = total_over_devices(sums, small)
+        grad_up, grad_down, grad_proj = finish(sums)
+        loss = jnp.sum(small[1]) / total
+        return (loss, grad_up[None], grad_down[None], small[None, 0], grad_proj[None])
 
     return jax.shard_map(
         body,

time: 623 us -> 513 us (0.82)
  waiting for transfers between devices: 232 us -> 0 us
  Pallas kernels: 351 us -> 508 us
  local copies, waits for them, and re-layouts: 20.5 us -> 0 us
  between operations: 15.8 us -> 2.43 us
    psum x1 -> x0, waiting for transfers between devices: 232 us -> none  [body(): sums = lax.psum(sums, all_axes)]
    pallas_call x1 -> x3, Pallas kernels: 68.7 us -> 226 us  [the longest x1 149 us: total_over_devices(): pl.pallas_call(total_kernel, out_shape=(jax.ShapeDtypeStruct(sums.shape,...]
    unnamed x2 -> x0, local copies, waits for them, and re-layouts: 10.7 us -> none
    broadcast_in_dim x1 -> x0, local copies, waits for them, and re-layouts: 9.81 us -> none  [body(): grad_proj = sums[2 * width:3 * width].T[None]]
  transfers between devices with their start and end apart: 1 -> 0, of which waited for: 1 -> 0; matrix products, arithmetic and copies ran while one was open for 0% -> 0% of each run, Pallas kernels for 0% -> 0%
where the time goes in v2:
time: 513 us
  Pallas kernels  508 us (99%)
    pallas_call x1, Pallas kernels, teacher_layer(): pl.pallas_call(teacher_kernel, out_shape=(jax.ShapeDtypeStruct((rows, wid...  282 us
    pallas_call x1, Pallas kernels, total_over_devices(): pl.pallas_call(total_kernel, out_shape=(jax.ShapeDtypeStruct(sums.shape,...  149 us
    pallas_call x1, Pallas kernels, student_layer(): pl.pallas_call(student_kernel, out_shape=(jax.ShapeDtypeStruct((3 * width...  67.8 us

profile of v2, /device:TPU:1, one launch (start us, length us, event | category | flops | bytes accessed | tf_op | source)
XLA Modules:
  0.0 512.5 jit_solution(16086914626031099021)
XLA Ops:
  0.6 282.2 %teacher.1 = (bf16[3072,2048]{1,0:T(8,128)(2,1)}, bf16[3,2048,2048]{2,1,0:T(8,128)(2,1)}, bf16[3,2048,2048]{2,1,0:T(8,128)(2,1)}, bf16[4,768,512]{2,1,0:T(8,128)(2,1)}) custom-call(bf16[3072,2048]{1,0:T(8,128)(2,1)} %bitcast.11, f32[1,2048]{1,0:T(1,128)} %gain_ref.2, bf16[2048,2048]{1,0:T(8,128)(2,1)} %bitcast.12, bf16[2048,2048]{1,0:T(8,128)(2,1)} %bitcast.13, ...), custom_call_target="tpu_custom_call" | custom-call | flops 206158430208 | bytes 67108864 | tf_op jit(solution)/shard_map/teacher/pallas_call | solution.py:264
  282.8 67.8 %student.1 = (f32[1536,2048]{1,0:T(8,128)}, f32[8,512]{1,0:T(8,128)}) custom-call(f32[1]{0:T(128)} %constant.1.clone.1.scale_ref, bf16[3072,2048]{1,0:T(8,128)(2,1)} %get-tuple-element.14.f_ref, bf16[3072,512]{1,0:T(8,128)(2,1)} %bitcast.21, f32[1,512]{1,0:T(1,128)} %gain_ref.3, bf16[512,2048]{1,0:T(8,128)(2,1)} %bitcast.18, bf16[2048,512]{1,0:T(8,128)(2,1)} %bitcast.19, ...), custom_call_target="tpu_custom_call" | custom-call | flops 51539607552 | bytes 15728640 | tf_op jit(solution)/shard_map/student/pallas_call | solution.py:345
  350.7 148.7 %total.1 = (f32[1536,2048]{1,0:T(8,128)}, f32[8,512]{1,0:T(8,128)}) custom-call(f32[1536,2048]{1,0:T(8,128)} %get-tuple-element.16.g_ref, f32[8,512]{1,0:T(8,128)} %get-tuple-element.17.small_ref), custom_call_target="tpu_custom_call" | custom-call | tf_op jit(solution)/shard_map/total/pallas_call | solution.py:481
  499.4 2.0 fusion
  502.0 9.4 %finish.1 = (f32[512,2048]{1,0:T(8,128)}, f32[2048,512]{1,0:T(8,128)}, f32[2048,512]{1,0:T(8,128)}) custom-call(f32[1536,2048]{1,0:T(8,128)} %get-tuple-element.19.up_ref.down_ref.proj_ref, f32[1536,2048]{1,0:T(8,128)} %get-tuple-element.19.up_ref.down_ref.proj_ref, f32[1536,2048]{1,0:T(8,128)} %get-tuple-element.19.up_ref.down_ref.proj_ref), custom_call_target="tpu_custom_call" | custom-call | tf_op jit(solution)/shard_map/finish/pallas_call | solution.py:513

commit v3 on v2

--- a/solution.py
+++ b/solution.py
@@ -13,8 +13,11 @@
 GELU_C = 0.044715
 TILE = 512
 CHUNK = 512
-PIECES = 8
-X_STEPS = (10, 20, 30, 40, 50, 60, 66, 70)
+PIECES = 4
+X_STEPS = (8, 18, 28, 38)
+Z_DIAG_STEP = 40
+STUDENT_STEP = 42
+Y_DIAG_STEPS = (44, 52)
 VMEM_LIMIT = 67043328
 
 
@@ -25,25 +28,33 @@
 def teacher_kernel(
     h_ref, gain_ref, w1_ref, w2_ref, s_ref,
     f_ref, w1g, w2g, sx_ref,
-    act, acc, w1_v, w2_v, u_a, u_b, s_v,
-    x_send, x_recv, y_send, y_recv, d_send, d_recv, g_send, g_recv, s_send, s_recv,
+    act, acc, w1_v, w2_v, p_a, p_b, u_a, u_b, s_v,
+    x_send, x_recv, y_send, y_recv, z_send, z_recv, yd_send, yd_recv, zd_send, zd_recv,
+    d_send, d_recv, g_send, g_recv, s_send, s_recv,
     w_sem, h_sem, f_sem, s_sem,
 ):
     data = lax.axis_index("data")
     model = lax.axis_index("model")
-    y_par = lax.rem(data, 2)
+    y_bit = lax.rem(data, 2)
+    z_bit = lax.rem(data // 2, 2)
     sib = (data, model + 1 - 2 * lax.rem(model, 2))
     x_nbr = (data, lax.rem(model + 2, 4))
-    y_nbr = (data + 1 - 2 * y_par, model)
+    y_nbr = (data + 1 - 2 * y_bit, model)
+    z_nbr = (data + 2 - 4 * z_bit, model)
     rows, width = act.shape
     quarter = w1_ref.shape[1]
-    half = quarter // 2
-    piece = half // PIECES
+    piece = CHUNK // PIECES
     n_tiles = rows // TILE
     per_quarter = quarter // CHUNK
     n_chunks = 4 * per_quarter
-    half_chunks = half // CHUNK
-    per_chunk = CHUNK // piece
+    chunk_x = 2 * y_bit + z_bit
+    chunk_y = 2 * (1 - y_bit) + z_bit
+    chunk_z = 2 * y_bit + 1 - z_bit
+    chunk_d = 3 - chunk_x
+    far = (chunk_x, chunk_y, chunk_z, chunk_d)
+
+    def cols(start, size):
+        return pl.ds(pl.multiple_of(start, size), size)
 
     def remote(src1, dst1, src2, dst2, send, recv, target):
         return (
@@ -51,27 +62,32 @@
             pltpu.make_async_remote_copy(src_ref=src2, dst_ref=dst2, send_sem=send.at[1], recv_sem=recv.at[1], device_id=target, device_id_type=MESH),
         )
 
-    def cols(start, size):
-        return pl.ds(pl.multiple_of(start, size), size)
+    def forward(chunk, p, send, recv, target):
+        where = cols(chunk * CHUNK + p * piece, piece)
+        return remote(w1g.at[1, :, where], w1g.at[1, :, where], w2g.at[1, where], w2g.at[1, where], send, recv, target)
 
     def x_copy(p):
-        where = cols(y_par * half + p * piece, piece)
+        where = cols(chunk_x * CHUNK + p * piece, piece)
         return remote(w1_ref.at[:, where], w1g.at[1, :, where], w2_ref.at[where], w2g.at[1, where], x_send.at[p], x_recv.at[p], x_nbr)
 
     def y_copy(p, mine):
-        where = cols((y_par if mine else 1 - y_par) * half + p * piece, piece)
-        return remote(w1g.at[1, :, where], w1g.at[1, :, where], w2g.at[1, where], w2g.at[1, where], y_send.at[p], y_recv.at[p], y_nbr)
+        return forward(chunk_x if mine else chunk_y, p, y_send.at[p], y_recv.at[p], y_nbr)
+
+    def z_copy(p, mine):
+        return forward(chunk_x if mine else chunk_z, p, z_send.at[p], z_recv.at[p], z_nbr)
+
+    def zd_copy(p, mine):
+        return forward(chunk_y if mine else chunk_d, p, zd_send.at[p], zd_recv.at[p], z_nbr)
+
+    def yd_copy(p, mine):
+        return forward(chunk_z if mine else chunk_d, p, yd_send.at[p - 2], yd_recv.at[p - 2], y_nbr)
 
     def d_copy(i):
         where = cols(i * CHUNK, CHUNK)
         return remote(w1_ref.at[:, where], w1g.at[0, :, where], w2_ref.at[where], w2g.at[0, where], d_send.at[i], d_recv.at[i], sib)
 
-    def far_cols(group):
-        side = y_par if group % 2 == 0 else 1 - y_par
-        return cols(side * half + (group // 2) * CHUNK, CHUNK)
-
     def g_copy(group):
-        where = far_cols(group)
+        where = cols(far[group] * CHUNK, CHUNK)
         return remote(w1g.at[1, :, where], w1g.at[2, :, where], w2g.at[1, where], w2g.at[2, where], g_send.at[group], g_recv.at[group], sib)
 
     def s_copy(k):
@@ -105,6 +121,14 @@
     def f_store(t):
         return pltpu.make_async_copy(act.at[tile_rows(t)], f_ref.at[tile_rows(t)], f_sem.at[t])
 
+    def take(copies):
+        for copy in copies:
+            copy.wait_recv()
+
+    def give(copies):
+        for copy in copies:
+            copy.start()
+
     for t in range(n_tiles):
         h_load(t).start()
     load(w1_ref.at[:, pl.ds(0, CHUNK)], w2_ref.at[pl.ds(0, CHUNK)], 0)
@@ -112,20 +136,19 @@
     own_in.start()
 
     barrier = pltpu.get_barrier_semaphore()
-    others = [(data, lax.rem(model + k, 4)) for k in (1, 2, 3)] + [y_nbr]
+    others = [(data, lax.rem(model + k, 4)) for k in (1, 2, 3)] + [y_nbr, z_nbr]
     for other in others:
         pl.semaphore_signal(barrier, inc=1, device_id=other, device_id_type=MESH)
     pl.semaphore_wait(barrier, len(others))
 
     for p in range(2):
-        for copy in x_copy(p):
-            copy.start()
+        give(x_copy(p))
     for i in range(per_quarter):
-        for copy in d_copy(i):
-            copy.start()
-
-    u_b[...] = jnp.zeros_like(u_b)
-    sub = 32
+        give(d_copy(i))
+
+    u_a[...] = jnp.zeros_like(u_a)
+    p_b[...] = jnp.zeros_like(p_b)
+    sub = 64
 
     @pl.loop(0, n_tiles)
     def _(t):
@@ -149,30 +172,43 @@
     def _(i):
         c = i // pairs
         j = lax.rem(i, pairs)
+        step = 2 * i
         slot = lax.rem(c, 2)
         first = 2 * j
-        before = lax.rem(first + n_tiles - 1, n_tiles)
+        before = lax.rem(first + n_tiles - 2, n_tiles)
         slot_before = jnp.where((j == 0) & (c > 0), 1 - slot, slot)
 
-        for p, step in enumerate(X_STEPS):
-
-            @pl.when(2 * i == step)
+        for p in range(PIECES):
+
+            @pl.when(step == X_STEPS[p])
             def _(p=p):
-                for copy in x_copy(p):
-                    copy.wait_recv()
-                for copy in y_copy(p, True):
-                    copy.start()
+                take(x_copy(p))
+                give(y_copy(p, True))
+                give(z_copy(p, True))
                 if p + 2 < PIECES:
-                    for copy in x_copy(p + 2):
-                        copy.start()
-                if p == PIECES - 2:
-                    for k in (1, 2, 3):
-                        s_copy(k).start()
-                if p % per_chunk == per_chunk - 1:
-                    for copy in g_copy(2 * (p // per_chunk)):
-                        copy.start()
-
-        @pl.when((j == 0))
+                    give(x_copy(p + 2))
+                if p == PIECES - 1:
+                    give(g_copy(0))
+
+        @pl.when(step == Z_DIAG_STEP)
+        def _():
+            for p in (0, 1):
+                take(y_copy(p, False))
+                give(zd_copy(p, True))
+
+        @pl.when(step == STUDENT_STEP)
+        def _():
+            for k in (1, 2, 3):
+                s_copy(k).start()
+
+        for p in (2, 3):
+
+            @pl.when(step == Y_DIAG_STEPS[p - 2])
+            def _(p=p):
+                take(z_copy(p, False))
+                give(yd_copy(p, True))
+
+        @pl.when(j == 0)
         def _():
             load_wait(slot)
 
@@ -188,45 +224,51 @@
 
             @pl.when(loads & (coming == per_quarter + k))
             def _(k=k):
-                for copy in d_copy(k):
-                    copy.wait_recv()
+                take(d_copy(k))
                 where = cols(k * CHUNK, CHUNK)
                 load(w1g.at[0, :, where], w2g.at[0, where], 1 - slot)
 
-        for group in range(per_quarter):
-            place = 2 * per_quarter + 2 * group
-
-            @pl.when(loads & (coming == place))
-            def _(group=group):
-                if group % 2 == 1:
-                    for q in range(per_chunk):
-                        for copy in y_copy((group // 2) * per_chunk + q, False):
-                            copy.wait_recv()
-                    for copy in g_copy(group):
-                        copy.start()
-                where = far_cols(group)
-                load(w1g.at[1, :, where], w2g.at[1, where], 1 - slot)
-
-            @pl.when(loads & (coming == place + 1))
-            def _(group=group):
-                for copy in g_copy(group):
-                    copy.wait_recv()
-                where = far_cols(group)
-                load(w1g.at[2, :, where], w2g.at[2, where], 1 - slot)
+        for place, (group, direct) in enumerate(((0, True), (0, False), (1, True), (2, True), (1, False), (2, False), (3, True), (3, False))):
+
+            @pl.when(loads & (coming == 2 * per_quarter + place))
+            def _(group=group, direct=direct):
+                if not direct:
+                    take(g_copy(group))
+                elif group == 1:
+                    for p in (2, 3):
+                        take(y_copy(p, False))
+                elif group == 2:
+                    for p in (0, 1):
+                        take(z_copy(p, False))
+                elif group == 3:
+                    for p in (0, 1):
+                        take(zd_copy(p, False))
+                    for p in (2, 3):
+                        take(yd_copy(p, False))
+                if direct and group:
+                    give(g_copy(group))
+                where = cols(far[group] * CHUNK, CHUNK)
+                source = 1 if direct else 2
+                load(w1g.at[source, :, where], w2g.at[source, where], 1 - slot)
 
         @pl.when((c == n_chunks - 1) & (j > 0))
         def _():
             h_load(first - 2).start()
             h_load(first - 1).start()
 
-        u_a[...] = gelu(jnp.dot(act[tile_rows(first), :], w1_v[slot], preferred_element_type=F32)).astype(BF16)
-        acc[tile_rows(before), :] += jnp.dot(u_b[...], w2_v[slot_before], preferred_element_type=F32)
-        u_b[...] = gelu(jnp.dot(act[tile_rows(first + 1), :], w1_v[slot], preferred_element_type=F32)).astype(BF16)
-        acc[tile_rows(first), :] += jnp.dot(u_a[...], w2_v[slot], preferred_element_type=F32)
+        p_a[...] = jnp.dot(act[tile_rows(first), :], w1_v[slot], preferred_element_type=F32)
+        u_b[...] = gelu(p_b[...]).astype(BF16)
+        acc[tile_rows(before), :] += jnp.dot(u_a[...], w2_v[slot_before], preferred_element_type=F32)
+        p_b[...] = jnp.dot(act[tile_rows(first + 1), :], w1_v[slot], preferred_element_type=F32)
+        u_a[...] = gelu(p_a[...]).astype(BF16)
+        acc[tile_rows(before + 1), :] += jnp.dot(u_b[...], w2_v[slot_before], preferred_element_type=F32)
 
     h_load(n_tiles - 2).start()
     h_load(n_tiles - 1).start()
-    acc[pl.ds((n_tiles - 1) * TILE, TILE), :] += jnp.dot(u_b[...], w2_v[(n_chunks - 1) % 2], preferred_element_type=F32)
+    last = (n_chunks - 1) % 2
+    u_b[...] = gelu(p_b[...]).astype(BF16)
+    acc[pl.ds((n_tiles - 2) * TILE, TILE), :] += jnp.dot(u_a[...], w2_v[last], preferred_element_type=F32)
+    acc[pl.ds((n_tiles - 1) * TILE, TILE), :] += jnp.dot(u_b[...], w2_v[last], preferred_element_type=F32)
 
     @pl.loop(0, n_tiles)
     def _(t):
@@ -244,11 +286,11 @@
         s_arrival(k).wait_recv()
         s_copy(k).wait_send()
     own_out.wait()
-    for p in range(PIECES):
-        for copy in x_copy(p) + y_copy(p, True):
-            copy.wait_send()
-    for i in range(per_quarter):
-        for copy in d_copy(i) + g_copy(i):
+    sent = [x_copy(p) + y_copy(p, True) + z_copy(p, True) for p in range(PIECES)]
+    sent += [d_copy(i) + g_copy(i) for i in range(per_quarter)]
+    sent += [zd_copy(p, True) + yd_copy(p + 2, True) for p in (0, 1)]
+    for copies in sent:
+        for copy in copies:
             copy.wait_send()
     for t in range(n_tiles):
         f_store(t).wait()
@@ -276,11 +318,14 @@
             pltpu.VMEM((rows, width), F32),
             pltpu.VMEM((2, width, CHUNK), BF16),
             pltpu.VMEM((2, CHUNK, width), BF16),
+            pltpu.VMEM((TILE, CHUNK), F32),
+            pltpu.VMEM((TILE, CHUNK), F32),
             pltpu.VMEM((TILE, CHUNK), BF16),
             pltpu.VMEM((TILE, CHUNK), BF16),
             pltpu.VMEM(student_rows.shape[1:], BF16),
-            dma((PIECES, 2)), dma((PIECES, 2)), dma((PIECES, 2)), dma((PIECES, 2)),
-            dma((per_quarter, 2)), dma((per_quarter, 2)), dma((per_quarter, 2)), dma((per_quarter, 2)),
+            *[dma((PIECES, 2))] * 6,
+            *[dma((2, 2))] * 4,
+            *[dma((per_quarter, 2))] * 4,
             dma((3,)), dma((3,)),
             dma((2, 2)), dma((n_tiles,)), dma((n_tiles,)), dma((2,)),
         ],
@@ -362,7 +407,7 @@
 
 def total_kernel(
     g_ref, small_ref, out_ref, small_out,
-    work, inbox, whole, small_v, small_in,
+    work, inbox, whole, packed, came_in, small_v, small_in,
     rs_send, rs_recv, ag_send, ag_recv, sm_send, sm_recv, in_sem, out_sem,
 ):
     data = lax.axis_index("data")
@@ -408,8 +453,13 @@
     def rs_copy(part, k):
         name = orders[part][k]
         gone = block(bases[part][k] + (1 - bits[name]) * sizes[k], sizes[k])
+        if k == 0:
+            source, target = work.at[gone], inbox.at[pl.ds(part * sizes[0], sizes[0])]
+        else:
+            where = pl.ds(part * sizes[0] + slots[k] - slots[1], sizes[k])
+            source, target = packed.at[where], came_in.at[where]
         return pltpu.make_async_remote_copy(
-            src_ref=work.at[gone], dst_ref=inbox.at[pl.ds(part * height + slots[k], sizes[k])],
+            src_ref=source, dst_ref=target,
             send_sem=rs_send.at[part, k], recv_sem=rs_recv.at[part, k], device_id=partner[name], device_id_type=MESH,
         )
 
@@ -442,10 +492,20 @@
             @pl.loop(0, sizes[k] // strip)
             def _(i, k=k, part=part, into=into):
                 kept = pl.ds(pl.multiple_of(bases[part][k + 1] + i * strip, strip), strip)
-                came = pl.ds(pl.multiple_of(part * height + slots[k] + i * strip, strip), strip)
-                into[kept, :] = work[kept, :] + inbox[came, :]
+                box, low = (inbox, 0) if k == 0 else (came_in, slots[k] - slots[1])
+                came = pl.ds(pl.multiple_of(part * sizes[0] + low + i * strip, strip), strip)
+                into[kept, :] = work[kept, :] + box[came, :].astype(F32)
 
             if k + 1 < stages:
+                name = orders[part][k + 1]
+                gone = bases[part][k + 1] + (1 - bits[name]) * sizes[k + 1]
+                low = part * sizes[0] + slots[k + 1] - slots[1]
+
+                @pl.loop(0, sizes[k + 1] // strip)
+                def _(i, gone=gone, low=low):
+                    source = pl.ds(pl.multiple_of(gone + i * strip, strip), strip)
+                    packed[pl.ds(pl.multiple_of(low + i * strip, strip), strip), :] = work[source, :].astype(BF16)
+
                 rs_copy(part, k + 1).start()
             else:
                 ag_copy(part, k, True).start()
@@ -485,8 +545,10 @@
         out_specs=(anywhere, vmem),
         scratch_shapes=[
             pltpu.VMEM((rows, width), F32),
+            pltpu.VMEM((rows // 2, width), F32),
             pltpu.VMEM((rows, width), F32),
-            pltpu.VMEM((rows, width), F32),
+            pltpu.VMEM((rows // 2, width), BF16),
+            pltpu.VMEM((rows // 2, width), BF16),
             pltpu.VMEM((5,) + small.shape, F32),
             pltpu.VMEM((5,) + small.shape, F32),
             dma((3, 5)), dma((3, 5)), dma((3, 5)), dma((3, 5)), dma((5,)), dma((5,)), dma((3,)), dma((3,)),

time: 513 us -> 470 us (0.916)
  Pallas kernels: 508 us -> 465 us
    pallas_call x1, Pallas kernels: 149 us -> 121 us  [total_over_devices(): pl.pallas_call(total_kernel, out_shape=(jax.ShapeDtypeStruct(sums.shape,...]
    pallas_call x1, Pallas kernels: 282 us -> 267 us  [teacher_layer(): pl.pallas_call(teacher_kernel, out_shape=(jax.ShapeDtypeStruct((rows, wid...]
where the time goes in v3:
time: 470 us
  Pallas kernels  465 us (99%)
    pallas_call x1, Pallas kernels, teacher_layer(): pl.pallas_call(teacher_kernel, out_shape=(jax.ShapeDtypeStruct((rows, wid...  267 us
    pallas_call x1, Pallas kernels, total_over_devices(): pl.pallas_call(total_kernel, out_shape=(jax.ShapeDtypeStruct(sums.shape,...  121 us
    pallas_call x1, Pallas kernels, student_layer(): pl.pallas_call(student_kernel, out_shape=(jax.ShapeDtypeStruct((3 * width...  67.8 us

profile of v3, /device:TPU:1, one launch (start us, length us, event | category | flops | bytes accessed | tf_op | source)
XLA Modules:
  0.0 469.6 jit_solution(947612848837235150)
XLA Ops:
  0.6 266.9 %teacher.1 = (bf16[3072,2048]{1,0:T(8,128)(2,1)}, bf16[3,2048,2048]{2,1,0:T(8,128)(2,1)}, bf16[3,2048,2048]{2,1,0:T(8,128)(2,1)}, bf16[4,768,512]{2,1,0:T(8,128)(2,1)}) custom-call(bf16[3072,2048]{1,0:T(8,128)(2,1)} %bitcast.11, f32[1,2048]{1,0:T(1,128)} %gain_ref.2, bf16[2048,2048]{1,0:T(8,128)(2,1)} %bitcast.12, bf16[2048,2048]{1,0:T(8,128)(2,1)} %bitcast.13, ...), custom_call_target="tpu_custom_call" | custom-call | flops 206158430208 | bytes 67108864 | tf_op jit(solution)/shard_map/teacher/pallas_call | solution.py:306
  267.5 67.8 %student.1 = (f32[1536,2048]{1,0:T(8,128)}, f32[8,512]{1,0:T(8,128)}) custom-call(f32[1]{0:T(128)} %constant.1.clone.1.scale_ref, bf16[3072,2048]{1,0:T(8,128)(2,1)} %get-tuple-element.14.f_ref, bf16[3072,512]{1,0:T(8,128)(2,1)} %bitcast.21, f32[1,512]{1,0:T(1,128)} %gain_ref.3, bf16[512,2048]{1,0:T(8,128)(2,1)} %bitcast.18, bf16[2048,512]{1,0:T(8,128)(2,1)} %bitcast.19, ...), custom_call_target="tpu_custom_call" | custom-call | flops 51539607552 | bytes 15728640 | tf_op jit(solution)/shard_map/student/pallas_call | solution.py:390
  335.4 121.1 %total.1 = (f32[1536,2048]{1,0:T(8,128)}, f32[8,512]{1,0:T(8,128)}) custom-call(f32[1536,2048]{1,0:T(8,128)} %get-tuple-element.16.g_ref, f32[8,512]{1,0:T(8,128)} %get-tuple-element.17.small_ref), custom_call_target="tpu_custom_call" | custom-call | tf_op jit(solution)/shard_map/total/pallas_call | solution.py:541
  456.5 2.0 fusion
  459.1 9.4 %finish.1 = (f32[512,2048]{1,0:T(8,128)}, f32[2048,512]{1,0:T(8,128)}, f32[2048,512]{1,0:T(8,128)}) custom-call(f32[1536,2048]{1,0:T(8,128)} %get-tuple-element.19.up_ref.down_ref.proj_ref, f32[1536,2048]{1,0:T(8,128)} %get-tuple-element.19.up_ref.down_ref.proj_ref, f32[1536,2048]{1,0:T(8,128)} %get-tuple-element.19.up_ref.down_ref.proj_ref), custom_call_target="tpu_custom_call" | custom-call | tf_op jit(solution)/shard_map/finish/pallas_call | solution.py:575

commit v4 on v3

--- a/solution.py
+++ b/solution.py
@@ -22,7 +22,8 @@
 
 
 def gelu(x):
-    return 0.5 * x * (1.0 + jnp.tanh(GELU_K * (x + GELU_C * (x * x * x))))
+    half = 0.5 * x
+    return half + half * jnp.tanh(x * (GELU_K + (GELU_K * GELU_C) * (x * x)))
 
 
 def teacher_kernel(
@@ -343,7 +344,7 @@
     return lax.dot_general(a, b, (((0,), (0,)), ((), ())), preferred_element_type=F32)
 
 
-def student_kernel(scale_ref, f_ref, s_ref, gain_ref, up_ref, down_ref, proj_ref, g_ref, small_ref, pre):
+def student_kernel(scale_ref, f_ref, s_ref, gain_ref, up_ref, down_ref, proj_ref, g_ref, small_ref, slope):
     i = pl.program_id(0)
     width = s_ref.shape[1]
     scale = scale_ref[0]
@@ -356,8 +357,12 @@
     state = s_ref[...].astype(F32)
     normed = state * lax.rsqrt(jnp.mean(state * state, axis=-1, keepdims=True) + EPS)
     act_in = (normed * gain_ref[...]).astype(BF16)
-    pre[...] = jnp.dot(act_in, up_ref[...], preferred_element_type=F32)
-    up_act = gelu(pre[...]).astype(BF16)
+    pre = jnp.dot(act_in, up_ref[...], preferred_element_type=F32)
+    half = 0.5 * pre
+    cubic = (GELU_K * GELU_C) * (pre * pre)
+    th = jnp.tanh(pre * (GELU_K + cubic))
+    up_act = (half + half * th).astype(BF16)
+    slope[...] = (0.5 + 0.5 * th) + (half * (1.0 - th * th)) * (GELU_K + 3.0 * cubic)
     new_state = (state + jnp.dot(up_act, down_ref[...], preferred_element_type=F32)).astype(BF16).astype(F32)
     target = jnp.dot(f_ref[...], proj_ref[...], preferred_element_type=F32).astype(BF16).astype(F32)
     inv = lax.rsqrt(jnp.mean(new_state * new_state, axis=-1, keepdims=True) + EPS)
@@ -369,11 +374,7 @@
     g_ref[pl.ds(2 * width, width), :] += scale * tn_dot(error.astype(BF16), f_ref[...])
     g_ref[pl.ds(width, width), :] += tn_dot(d_out, up_act)
     d_up = nt_dot(d_out, down_ref[...])
-    x = pre[...]
-    x2 = x * x
-    th = jnp.tanh(GELU_K * (x + GELU_C * (x2 * x)))
-    slope = 0.5 * (1.0 + th) + 0.5 * x * (1.0 - th * th) * (GELU_K * (1.0 + 3.0 * GELU_C * x2))
-    d_pre = (slope * d_up).astype(BF16)
+    d_pre = (slope[...] * d_up).astype(BF16)
     g_ref[pl.ds(0, width), :] += tn_dot(act_in, d_pre)
     d_act = nt_dot(d_pre, up_ref[...])
     small_ref[pl.ds(0, 1), :] += jnp.sum(d_act * normed, axis=0, keepdims=True)

time: 470 us -> 468 us (level)
  no operation moved by 1% of the time
where the time goes in v4:
time: 468 us
  Pallas kernels  463 us (99%)
    pallas_call x1, Pallas kernels, teacher_layer(): pl.pallas_call(teacher_kernel, out_shape=(jax.ShapeDtypeStruct((rows, wid...  264 us
    pallas_call x1, Pallas kernels, total_over_devices(): pl.pallas_call(total_kernel, out_shape=(jax.ShapeDtypeStruct(sums.shape,...  121 us
    pallas_call x1, Pallas kernels, student_layer(): pl.pallas_call(student_kernel, out_shape=(jax.ShapeDtypeStruct((3 * width...  68.7 us
    pallas_call x1, Pallas kernels, finish(): pl.pallas_call(finish_kernel, out_shape=(flat, tall, tall), grid=(wide //...  9.37 us

profile of v4, /device:TPU:1, one launch (start us, length us, event | category | flops | bytes accessed | tf_op | source)
XLA Modules:
  0.0 467.7 jit_solution(6421743748753147766)
XLA Ops:
  0.6 264.2 %teacher.1 = (bf16[3072,2048]{1,0:T(8,128)(2,1)}, bf16[3,2048,2048]{2,1,0:T(8,128)(2,1)}, bf16[3,2048,2048]{2,1,0:T(8,128)(2,1)}, bf16[4,768,512]{2,1,0:T(8,128)(2,1)}) custom-call(bf16[3072,2048]{1,0:T(8,128)(2,1)} %bitcast.11, f32[1,2048]{1,0:T(1,128)} %gain_ref.2, bf16[2048,2048]{1,0:T(8,128)(2,1)} %bitcast.12, bf16[2048,2048]{1,0:T(8,128)(2,1)} %bitcast.13, ...), custom_call_target="tpu_custom_call" | custom-call | flops 206158430208 | bytes 67108864 | tf_op jit(solution)/shard_map/teacher/pallas_call | solution.py:307
  264.8 68.7 %student.1 = (f32[1536,2048]{1,0:T(8,128)}, f32[8,512]{1,0:T(8,128)}) custom-call(f32[1]{0:T(128)} %constant.1.clone.1.scale_ref, bf16[3072,2048]{1,0:T(8,128)(2,1)} %get-tuple-element.14.f_ref, bf16[3072,512]{1,0:T(8,128)(2,1)} %bitcast.21, f32[1,512]{1,0:T(1,128)} %gain_ref.3, bf16[512,2048]{1,0:T(8,128)(2,1)} %bitcast.18, bf16[2048,512]{1,0:T(8,128)(2,1)} %bitcast.19, ...), custom_call_target="tpu_custom_call" | custom-call | flops 51539607552 | bytes 15728640 | tf_op jit(solution)/shard_map/student/pallas_call | solution.py:391
  333.5 121.2 %total.1 = (f32[1536,2048]{1,0:T(8,128)}, f32[8,512]{1,0:T(8,128)}) custom-call(f32[1536,2048]{1,0:T(8,128)} %get-tuple-element.16.g_ref, f32[8,512]{1,0:T(8,128)} %get-tuple-element.17.small_ref), custom_call_target="tpu_custom_call" | custom-call | tf_op jit(solution)/shard_map/total/pallas_call | solution.py:542
  454.6 2.0 fusion
  457.2 9.4 %finish.1 = (f32[512,2048]{1,0:T(8,128)}, f32[2048,512]{1,0:T(8,128)}, f32[2048,512]{1,0:T(8,128)}) custom-call(f32[1536,2048]{1,0:T(8,128)} %get-tuple-element.19.up_ref.down_ref.proj_ref, f32[1536,2048]{1,0:T(8,128)} %get-tuple-element.19.up_ref.down_ref.proj_ref, f32[1536,2048]{1,0:T(8,128)} %get-tuple-element.19.up_ref.down_ref.proj_ref), custom_call_target="tpu_custom_call" | custom-call | tf_op jit(solution)/shard_map/finish/pallas_call | solution.py:576
